TPU v7x, 256 devices: a whole 4x4x8 slice. The times are simulated.
256 devices in a mesh: dp: 8 (over z), expert: 32 (over x, y, core).
Axes of the slice: x: 4, y: 4, z: 8, core: 2. Of those that a mesh axis runs over, the one named last changes fastest.
Arguments:
- tokens: bfloat16 [2048, 7168], P('expert'), may hold values from -6 to 6
- routes: int32 [2048, 8], P('expert'), may hold values from 0 to 31, all different within a row; in each aligned block of 64 rows (0 to 63, 64 to 127, ...) at most 20 rows name the same one
- route_weight: int32 [2048, 8], P('expert'), may hold values from 1 to 4096
- w_gate: bfloat16 [32, 7168, 2048], P('expert', None, 'dp'), may hold values from -0.0625 to 0.0625
- w_up: bfloat16 [32, 7168, 2048], P('expert', None, 'dp'), may hold values from -0.0625 to 0.0625
- w_down: bfloat16 [32, 2048, 7168], P('expert', 'dp'), may hold values from -0.125 to 0.125
- prev_inputs: bfloat16 [8, 32, 64, 7168], P('dp', 'expert'), may hold values from -6 to 6
Outputs:
- mixed: bfloat16 [2048, 7168], P('expert', 'dp')
- hessian: float32 [7168, 32, 128], P('dp', 'expert')
Inputs may be any that keep to these rules, and one draw needn't show every extreme that they name: `routes`: in each aligned block of 64 rows (the rows of one index of expert) no expert is named more than 20 times, a bound that some block reaches; the 8 experts of a token differ.
All inputs are finite; a program needn't handle non-finite values.
Results may differ from a plain program's by a relative error of at most 0.014.
Values may be sent and summed in bfloat16 or wider, within the bound.
A program may use at most 128 MiB of HBM per device.

v0:
```python
import jax
import jax.numpy as jnp
from jax import lax
from jax.sharding import PartitionSpec as P

HESS_COLS = 128


def split_up(value, dim, length):
    before, after = (value.shape[:dim], value.shape[dim + 1 :])
    return jnp.moveaxis(value.reshape(*before, length, -1, *after), dim, 0)


def summed_on_arrival(value, axis, dim):
    blocks = split_up(value, dim, lax.axis_size(axis))
    arrived = lax.all_to_all(blocks, axis, split_axis=0, concat_axis=0, tiled=True)
    return arrived.astype(jnp.float32).sum(axis=0)


def route_slots(flat_ids, experts_all):
    onehot = (flat_ids[:, None] == jnp.arange(experts_all, dtype=jnp.int32)[None, :]).astype(
        jnp.int32
    )
    earlier = jnp.cumsum(onehot, axis=0) - onehot
    return jnp.sum(earlier * onehot, axis=1)


def combine_rows(back, places, shares, tok_dev, top):
    columns = back.shape[-1]
    rows = back.reshape(-1, columns)[places]
    weighted = rows.astype(jnp.float32) * shares.reshape(-1, 1)
    return jnp.sum(weighted.reshape(tok_dev, top, columns), axis=1)


def shards(tokens, routes, route_weight, w_gate, w_up, w_down, prev_inputs):
    tok_dev, top = routes.shape
    exp_dev = w_gate.shape[0]
    width = tokens.shape[1]
    n_expert = lax.axis_size("expert")
    n_dp = lax.axis_size("dp")
    experts_all = exp_dev * n_expert
    capacity = min(tok_dev, tok_dev * top * 5 // (4 * experts_all))
    col_width = width // n_dp
    flat_ids = routes.reshape(-1)
    slots = route_slots(flat_ids, experts_all)
    places = flat_ids * capacity + slots
    weight_counts = route_weight.astype(jnp.float32)
    shares = 2.5 * weight_counts / jnp.sum(weight_counts, axis=1, keepdims=True)
    picks = jnp.arange(experts_all * capacity, dtype=jnp.int32)[:, None] == places[None, :]
    placing = jnp.any(picks.reshape(experts_all * capacity, tok_dev, top), axis=2).astype(
        jnp.bfloat16
    )
    my_cols = lax.dynamic_slice_in_dim(tokens, lax.axis_index("dp") * col_width, col_width, 1)
    outgoing = jnp.dot(placing, my_cols, preferred_element_type=jnp.float32).astype(jnp.bfloat16)
    outgoing = outgoing.reshape(experts_all, capacity, col_width)
    arrived = lax.all_to_all(outgoing, "expert", split_axis=0, concat_axis=0, tiled=True)
    arrived = arrived.reshape(n_expert, exp_dev, capacity, col_width)
    piece = lax.all_gather(arrived, "dp", axis=3, tiled=True)
    gate_add = jnp.einsum("sjcd,jdf->sjcf", piece, w_gate, preferred_element_type=jnp.float32)
    up_add = jnp.einsum("sjcd,jdf->sjcf", piece, w_up, preferred_element_type=jnp.float32)
    history = prev_inputs.reshape(prev_inputs.shape[1], prev_inputs.shape[2], width)
    head_cols = history[:, :, :HESS_COLS]
    gram_scale = 2.0 / (n_dp * history.shape[1])
    hessian = lax.psum_scatter(
        (
            jnp.einsum("jrd,jrh->djh", history, head_cols, preferred_element_type=jnp.float32)
            * gram_scale
        ).astype(jnp.bfloat16),
        "dp",
        scatter_dimension=0,
        tiled=True,
    ).astype(jnp.float32)
    hidden = (jax.nn.silu(gate_add) * up_add).astype(jnp.bfloat16)
    partial_out = jnp.einsum("sjcf,jfd->sjcd", hidden, w_down, preferred_element_type=jnp.float32)
    partial_out = partial_out.astype(jnp.bfloat16)
    back = lax.all_to_all(
        partial_out.reshape(experts_all, capacity, width),
        "expert",
        split_axis=0,
        concat_axis=0,
        tiled=True,
    )
    own_sum = combine_rows(back, places, shares, tok_dev, top)
    mixed = summed_on_arrival(own_sum.astype(jnp.bfloat16), "dp", 1)
    return (mixed.astype(jnp.bfloat16), hessian)


def solution(mesh):
    placed = (
        P("expert", None),
        P("expert", None),
        P("expert", None),
        P("expert", None, "dp"),
        P("expert", None, "dp"),
        P("expert", "dp", None),
        P("dp", "expert", None, None),
    )
    return jax.shard_map(
        shards,
        mesh=mesh,
        in_specs=placed,
        out_specs=(P("expert", "dp"), P("dp", "expert", None)),
        check_vma=False,
    )
```

profile of v0, /device:TPU:13, one launch (start us, length us, event | category | flops | bytes accessed | tf_op | source)
XLA Modules:
  0.0 430.2 jit_solution(2899087094357470166)
XLA Ops:
  7.2 0.0 copy-start
  7.2 0.0 all-gather.3.cloned.1.call-start
  7.2 0.8 copy.38
  8.1 0.1 eq.44
  8.2 0.1 eq.40
  8.3 1.2 reduce-window.6
  9.4 0.2 slice_reduce_fusion
  9.7 0.1 fusion.28
  9.8 0.1 reduce_sum.44
  9.9 0.5 fusion.8
  10.4 0.0 copy-done
  10.4 0.5 convolution_convert_fusion.1
  10.9 0.3 reshape.127
  11.2 25.7 %all_to_all.15 = bf16[32,20,896]{2,1,0:T(8,128)(2,1)S(1)} all-to-all(bf16[32,20,896]{2,1,0:T(8,128)(2,1)S(1)} %reshape.127), channel_id=1, replica_groups=mesh['dp'=8,'expert'=32] {'expert'}, dimensions={0} | all-to-all | bytes 2293760 | tf_op jit(solution)/shard_map/all_to_all | solution.py:56
  36.9 1.1 copy.42
  38.1 0.0 all-gather.3.cloned.1.call-update
  38.1 102.8 %all-gather.3.cloned.1.call-done = bf16[32,20,7168]{2,0,1:T(8,128)(2,1)} async-done(((bf16[32,20,896]{2,0,1:T(8,128)(2,1)}), bf16[32,20,7168]{2,0,1:T(8,128)(2,1)}) %all-gather.3.cloned.1.call-update) | async-done | bytes 9175056 | tf_op jit(solution)/shard_map/all_gather | solution.py:58
  140.9 7.3 %fusion.9 = f32[32,1,20,256]{3,0,2,1:T(8,128)S(1)} fusion(bf16[32,20,7168]{2,0,1:T(8,128)(2,1)} %all-gather.3.cloned.1.call-done, bf16[1,7168,256]{2,1,0:T(8,128)(2,1)} %param.10), kind=kOutput, calls=%fused_computation.15 | convolution fusion | flops 2348810240 | bytes 13500416 | tf_op jit(solution)/shard_map/sjcd,jdf->sjcf/dot_general | solution.py:59
  148.2 0.0 copy-done.5
  148.2 1.0 copy-done.6
  149.2 2.5 fusion.21
  151.7 0.0 copy-done.2
  151.8 6.1 %convolution_convert_fusion = bf16[32,20,7168]{2,0,1:T(8,128)(2,1)} fusion(bf16[32,20,256]{2,0,1:T(8,128)(2,1)S(1)} %fusion.21, bf16[1,256,7168]{2,1,0:T(8,128)(2,1)S(1)} %copy-done.2), kind=kOutput, calls=%fused_computation.3 | convolution fusion | flops 2353397760 | bytes 13172736 | tf_op jit(solution)/shard_map/sjcf,jfd->sjcd/dot_general | solution.py:74
  157.8 13.0 %copy.43 = bf16[32,20,7168]{2,1,0:T(8,128)(2,1)} copy(bf16[32,20,7168]{2,0,1:T(8,128)(2,1)} %convolution_convert_fusion) | data formatting | bytes 18350080 | tf_op jit(solution)/shard_map/convert_element_type | solution.py:75
  170.8 8.0 %all-to-all-start.1 = ((bf16[32,20,7168]{2,1,0:T(8,128)(2,1)}), bf16[32,20,7168]{2,1,0:T(8,128)(2,1)}, u32[]{:S(2)}, u32[]{:S(2)}) async-start(bf16[32,20,7168]{2,1,0:T(8,128)(2,1)} %copy.43), calls=%async_computation.1 | async-start | bytes 22020096 | tf_op jit(solution)/shard_map/all_to_all | solution.py:76
  178.9 0.0 reduce-scatter.4.cloned.1.call-start
  178.9 0.0 copy-done.3
  178.9 0.0 copy-start.4
  178.9 0.7 fusion.2
  179.6 2.3 copy.49
  181.9 0.0 reduce-scatter.4.cloned.1.call-update
  182.0 0.1 mul.62
  182.0 0.0 copy-done.4
  182.1 0.1 copy.44
  182.2 167.9 %all-to-all-done.1 = bf16[32,20,7168]{2,1,0:T(8,128)(2,1)} async-done(((bf16[32,20,7168]{2,1,0:T(8,128)(2,1)}), bf16[32,20,7168]{2,1,0:T(8,128)(2,1)}, u32[]{:S(2)}, u32[]{:S(2)}) %all-to-all-start.1) | async-done | bytes 9175072 | tf_op jit(solution)/shard_map/all_to_all | solution.py:76
  350.1 13.3 %reshape.134 = bf16[640,7168]{1,0:T(8,128)(2,1)} reshape(bf16[32,20,7168]{2,1,0:T(8,128)(2,1)} %all-to-all-done.1) | data formatting | bytes 18350080 | tf_op jit(solution)/shard_map/reshape | solution.py:30
  363.4 18.6 %gather_fusion = bf16[512,7168]{1,0:T(8,128)(2,1)} fusion(bf16[640,7168]{1,0:T(8,128)(2,1)} %reshape.134, s32[1024]{0:T(1024)S(1)} %pad_clamp_fusion), kind=kCustom, calls=%fused_computation | custom fusion | bytes 14682112 | tf_op jit(solution)/shard_map/gather | solution.py:30
  382.0 8.9 %fusion = bf16[64,7168]{1,0:T(8,128)(2,1)S(1)} fusion(bf16[512,7168]{1,0:T(8,128)(2,1)} %gather_fusion, f32[64,8]{1,0:T(8,128)S(1)} %copy.44), kind=kLoop, calls=%fused_computation.2 | loop fusion | flops 10551296 | bytes 8259584 | tf_op jit(solution)/shard_map/reduce_sum | solution.py:32
  390.9 0.0 copy-start.1
  390.9 0.1 copy.52
  391.1 1.1 copy.45
  392.1 4.0 all-to-all-start.2
  396.2 0.0 reduce-scatter.4.cloned.1.call-done
  396.2 1.1 copy.50
  397.3 1.1 copy.46
  398.4 24.2 %all-to-all-done.2 = bf16[8,64,896]{2,1,0:T(8,128)(2,1)S(1)} async-done(((bf16[8,64,896]{2,1,0:T(8,128)(2,1)}), bf16[8,64,896]{2,1,0:T(8,128)(2,1)S(1)}, u32[]{:S(2)}, u32[]{:S(2)}) %all-to-all-start.2) | async-done | bytes 917536 | tf_op jit(solution)/shard_map/all_to_all | solution.py:16
  422.6 0.8 reduce_sum.48
  423.3 0.0 copy-done.1
  (13 shorter events, 0.1 us)
Async XLA Ops:
  7.2 3.2 copy-start
  7.2 133.7 %all-gather.3.cloned.1.call-start = ((), (), s32[]{:S(2)}) async-start(), calls=%async_computation.4 | async-start | bytes 10321920 | tf_op jit(solution)/shard_map/all_gather | solution.py:58
  140.9 7.3 %copy-start.5 = (bf16[32,20,7168]{2,0,1:T(8,128)(2,1)S(1)}, bf16[32,20,7168]{2,0,1:T(8,128)(2,1)}, u32[]{:S(2)}) copy-start(bf16[32,20,7168]{2,0,1:T(8,128)(2,1)} %all-gather.3.cloned.1.call-done) | copy-start | bytes 27525124
  140.9 8.3 %copy-start.6 = (bf16[1,7168,256]{2,1,0:T(8,128)(2,1)S(1)}, bf16[1,7168,256]{2,1,0:T(8,128)(2,1)}, u32[]{:S(2)}) copy-start(bf16[1,7168,256]{2,1,0:T(8,128)(2,1)} %param.11) | copy-start | bytes 11010052
  149.2 2.5 copy-start.2
  170.8 8.1 %copy-start.3 = (bf16[1,1,64,7168]{3,2,1,0:T(8,128)(2,1)S(1)}, bf16[1,1,64,7168]{3,2,1,0:T(8,128)(2,1)}, u32[]{:S(2)}) copy-start(bf16[1,1,64,7168]{3,2,1,0:T(8,128)(2,1)} %param.13) | copy-start | bytes 2752516
  170.8 179.2 %all-to-all-start.1 = ((bf16[32,20,7168]{2,1,0:T(8,128)(2,1)}), bf16[32,20,7168]{2,1,0:T(8,128)(2,1)}, u32[]{:S(2)}, u32[]{:S(2)}) async-start(bf16[32,20,7168]{2,1,0:T(8,128)(2,1)} %copy.43), calls=%async_computation.1 | async-start | bytes 22020096 | tf_op jit(solution)/shard_map/all_to_all | solution.py:76
  178.9 217.3 %reduce-scatter.4.cloned.1.call-start = ((), (), s32[]{:S(2)}) async-start(), calls=%async_computation.5 | async-start | bytes 2064384
  178.9 3.1 copy-start.4
  390.9 32.4 %copy-start.1 = (bf16[64,7168]{1,0:T(8,128)(2,1)S(1)}, bf16[64,7168]{1,0:T(8,128)(2,1)}, u32[]{:S(2)}) copy-start(bf16[64,7168]{1,0:T(8,128)(2,1)} %param.7) | copy-start | bytes 2752516
  392.1 30.4 %all-to-all-start.2 = ((bf16[8,64,896]{2,1,0:T(8,128)(2,1)}), bf16[8,64,896]{2,1,0:T(8,128)(2,1)S(1)}, u32[]{:S(2)}, u32[]{:S(2)}) async-start(bf16[8,64,896]{2,1,0:T(8,128)(2,1)} %copy.45), calls=%async_computation.2 | async-start | bytes 1835008 | tf_op jit(solution)/shard_map/all_to_all | solution.py:16
Sparse Core Ops, SparseCore 0:
  38.2 102.6 all-gather.2
  182.2 35.9 reduce-scatter.3
where the time goes:
time: 431 us; the launch traced here: 430 us
  waiting for transfers between devices  295 us (68%)
  local copies, waits for them, and re-layouts  54.5 us (13%)
  blocking collectives  25.7 us (6%)
  matrix products  17.1 us (4%)
  between operations  14.2 us (3%)
  starting transfers between devices  12.1 us (3%)
  other arithmetic  11.6 us (3%)
    all_to_all x1, waiting for transfers between devices, shards(): lax.all_to_all(partial_out.reshape(experts_all, capacity, width), 'expert...  168 us
    all_gather x1, waiting for transfers between devices, shards(): piece = lax.all_gather(arrived, 'dp', axis=3, tiled=True)  103 us
    all_to_all x1, blocking collectives, shards(): lax.all_to_all(outgoing, 'expert', split_axis=0, concat_axis=0, tiled=True)  25.7 us
    all_to_all x1, waiting for transfers between devices, summed_on_arrival(): lax.all_to_all(blocks, axis, split_axis=0, concat_axis=0, tiled=True)  24.2 us
    gather x1, local copies, waits for them, and re-layouts, combine_rows(): rows = back.reshape(-1, columns)[places]  18.6 us
    reshape x1, local copies, waits for them, and re-layouts, combine_rows(): rows = back.reshape(-1, columns)[places]  13.3 us
    convert_element_type x1, local copies, waits for them, and re-layouts, shards(): partial_out = partial_out.astype(jnp.bfloat16)  13 us
    reduce_sum x1, other arithmetic, combine_rows(): return jnp.sum(weighted.reshape(tok_dev, top, columns), axis=1)  8.91 us
  transfers between devices with their start and end apart: 4, of which 3 were waited for; matrix products, arithmetic and copies ran while one was open for 11% of the time, Pallas kernels for 0%

commit v1 on v0

--- a/solution.py
+++ b/solution.py
@@ -55,7 +55,9 @@
     outgoing = outgoing.reshape(experts_all, capacity, col_width)
     arrived = lax.all_to_all(outgoing, "expert", split_axis=0, concat_axis=0, tiled=True)
     arrived = arrived.reshape(n_expert, exp_dev, capacity, col_width)
-    piece = lax.all_gather(arrived, "dp", axis=3, tiled=True)
+    piece = jnp.concatenate(
+        lax.all_to_all(jnp.stack([arrived] * lax.axis_size("dp")), "dp", 0, 0), axis=3
+    )
     gate_add = jnp.einsum("sjcd,jdf->sjcf", piece, w_gate, preferred_element_type=jnp.float32)
     up_add = jnp.einsum("sjcd,jdf->sjcf", piece, w_up, preferred_element_type=jnp.float32)
     history = prev_inputs.reshape(prev_inputs.shape[1], prev_inputs.shape[2], width)

time: 431 us -> 574 us (1.33); the launches traced: 430 us -> 567 us
  blocking collectives: 25.7 us -> 237 us
  waiting for transfers between devices: 295 us -> 194 us
  local copies, waits for them, and re-layouts: 54.5 us -> 81.2 us
    all_to_all x0 -> x1, blocking collectives: none -> 211 us  [shards(): lax.all_to_all(jnp.stack([arrived] * lax.axis_size('dp')), 'dp', 0, 0)]
    all_gather x1 -> x0, waiting for transfers between devices: 103 us -> none  [shards(): piece = lax.all_gather(arrived, 'dp', axis=3, tiled=True)]
    another operation x1 -> x3, local copies, waits for them, and re-layouts: 0.01 us -> 15.3 us
    reshape x0 -> x1, local copies, waits for them, and re-layouts: none -> 12.4 us  [shards(): jnp.concatenate(lax.all_to_all(jnp.stack([arrived] * lax.axis_size('dp'))...]
  transfers between devices with their start and end apart: 4 -> 3, of which waited for: 3 -> 2; matrix products, arithmetic and copies ran while one was open for 11% -> 8% of each run, Pallas kernels for 0% -> 0%
where the time goes in v1:
time: 574 us; the launch traced here: 567 us
  blocking collectives  237 us (41%)
  waiting for transfers between devices  194 us (34%)
  local copies, waits for them, and re-layouts  81.2 us (14%)
  matrix products  17.1 us (3%)
  between operations  14.5 us (3%)
  starting transfers between devices  11.8 us (2%)
  other arithmetic  11.6 us (2%)
    all_to_all x1, blocking collectives, shards(): lax.all_to_all(jnp.stack([arrived] * lax.axis_size('dp')), 'dp', 0, 0)  211 us
    all_to_all x1, waiting for transfers between devices, shards(): lax.all_to_all(partial_out.reshape(experts_all, capacity, width), 'expert...  169 us
    all_to_all x1, blocking collectives, shards(): lax.all_to_all(outgoing, 'expert', split_axis=0, concat_axis=0, tiled=True)  25.7 us
    all_to_all x1, waiting for transfers between devices, summed_on_arrival(): lax.all_to_all(blocks, axis, split_axis=0, concat_axis=0, tiled=True)  24.1 us
    gather x1, local copies, waits for them, and re-layouts, combine_rows(): rows = back.reshape(-1, columns)[places]  18.8 us
    another operation x2, local copies, waits for them, and re-layouts  14.4 us
    reshape x1, local copies, waits for them, and re-layouts, combine_rows(): rows = back.reshape(-1, columns)[places]  13.3 us
    convert_element_type x1, local copies, waits for them, and re-layouts, shards(): partial_out = partial_out.astype(jnp.bfloat16)  12.8 us
  transfers between devices with their start and end apart: 3, of which 2 were waited for; matrix products, arithmetic and copies ran while one was open for 8% of the time, Pallas kernels for 0%

profile of v1, /device:TPU:13, one launch (start us, length us, event | category | flops | bytes accessed | tf_op | source)
XLA Modules:
  0.0 566.9 jit_solution(2728425536888815909)
XLA Ops:
  7.2 0.0 copy-start
  7.2 0.9 copy.40
  8.0 0.1 eq.44
  8.1 0.1 eq.40
  8.2 1.2 reduce-window.6
  9.4 0.2 slice_reduce_fusion
  9.7 0.1 fusion.28
  9.8 0.1 reduce_sum.44
  9.9 0.5 fusion.8
  10.4 0.0 copy-done
  10.4 0.5 convolution_convert_fusion.1
  10.9 0.3 reshape.132
  11.2 25.7 %all_to_all.20 = bf16[32,20,896]{2,1,0:T(8,128)(2,1)S(1)} all-to-all(bf16[32,20,896]{2,1,0:T(8,128)(2,1)S(1)} %reshape.132), channel_id=1, replica_groups=mesh['dp'=8,'expert'=32] {'expert'}, dimensions={0} | all-to-all | bytes 2293760 | tf_op jit(solution)/shard_map/all_to_all | solution.py:56
  36.9 0.1 copy.44
  37.0 0.9 stack.3
  37.9 211.5 %all_to_all.21 = bf16[8,32,1,20,896]{4,1,3,2,0:T(8,128)(2,1)} all-to-all(bf16[8,32,1,20,896]{4,1,3,2,0:T(8,128)(2,1)S(1)} %stack.3), channel_id=1, replica_groups=mesh['dp'=8,'expert'=32] {'dp'}, dimensions={0} | all-to-all | bytes 18350080 | tf_op jit(solution)/shard_map/all_to_all | solution.py:59
  249.4 12.4 %copy.45 = bf16[32,1,20,8,896]{4,3,0,2,1:T(8,128)(2,1)} copy(bf16[32,1,20,8,896]{4,0,2,1,3:T(8,128)(2,1)} %bitcast.95) | data formatting | bytes 18350080 | tf_op jit(solution)/shard_map/reshape | solution.py:58
  261.8 14.4 %reshape.134 = bf16[32,20,7168]{2,0,1:T(8,128)(2,1)} reshape(bf16[32,1,20,8,896]{4,3,0,2,1:T(8,128)(2,1)} %copy.45) | data formatting | bytes 18350080 | tf_op jit(solution)/shard_map/reshape.5
  276.2 0.0 copy-start.2
  276.2 0.0 copy-start.6
  276.2 7.3 %fusion.9 = f32[32,1,20,256]{3,0,2,1:T(8,128)S(1)} fusion(bf16[32,20,7168]{2,0,1:T(8,128)(2,1)} %reshape.134, bf16[1,7168,256]{2,1,0:T(8,128)(2,1)} %param.10), kind=kOutput, calls=%fused_computation.15 | convolution fusion | flops 2348810240 | bytes 13500416 | tf_op jit(solution)/shard_map/sjcd,jdf->sjcf/dot_general | solution.py:61
  283.5 0.0 copy-done.2
  283.5 0.9 copy-done.6
  284.5 2.5 fusion.21
  287.0 0.0 copy-done.3
  287.0 6.1 %convolution_convert_fusion = bf16[32,20,7168]{2,0,1:T(8,128)(2,1)} fusion(bf16[32,20,256]{2,0,1:T(8,128)(2,1)S(1)} %fusion.21, bf16[1,256,7168]{2,1,0:T(8,128)(2,1)S(1)} %copy-done.3), kind=kOutput, calls=%fused_computation.3 | convolution fusion | flops 2353397760 | bytes 13172736 | tf_op jit(solution)/shard_map/sjcf,jfd->sjcd/dot_general | solution.py:76
  293.1 12.8 %copy.46 = bf16[32,20,7168]{2,1,0:T(8,128)(2,1)} copy(bf16[32,20,7168]{2,0,1:T(8,128)(2,1)} %convolution_convert_fusion) | data formatting | bytes 18350080 | tf_op jit(solution)/shard_map/convert_element_type | solution.py:77
  305.9 8.2 %all-to-all-start.2 = ((bf16[32,20,7168]{2,1,0:T(8,128)(2,1)}), bf16[32,20,7168]{2,1,0:T(8,128)(2,1)}, u32[]{:S(2)}, u32[]{:S(2)}) async-start(bf16[32,20,7168]{2,1,0:T(8,128)(2,1)} %copy.46), calls=%async_computation.2 | async-start | bytes 22020096 | tf_op jit(solution)/shard_map/all_to_all | solution.py:78
  314.1 0.0 reduce-scatter.4.cloned.1.call-start
  314.2 0.0 copy-start.5
  314.2 0.7 fusion.2
  314.9 2.3 copy.52
  317.2 0.0 reduce-scatter.4.cloned.1.call-update
  317.2 0.1 mul.62
  317.3 0.1 copy.47
  317.5 169.5 %all-to-all-done.2 = bf16[32,20,7168]{2,1,0:T(8,128)(2,1)} async-done(((bf16[32,20,7168]{2,1,0:T(8,128)(2,1)}), bf16[32,20,7168]{2,1,0:T(8,128)(2,1)}, u32[]{:S(2)}, u32[]{:S(2)}) %all-to-all-start.2) | async-done | bytes 9175072 | tf_op jit(solution)/shard_map/all_to_all | solution.py:78
  486.9 13.3 %reshape.139 = bf16[640,7168]{1,0:T(8,128)(2,1)} reshape(bf16[32,20,7168]{2,1,0:T(8,128)(2,1)} %all-to-all-done.2) | data formatting | bytes 18350080 | tf_op jit(solution)/shard_map/reshape | solution.py:30
  500.2 18.8 %gather_fusion = bf16[512,7168]{1,0:T(8,128)(2,1)} fusion(bf16[640,7168]{1,0:T(8,128)(2,1)} %reshape.139, s32[1024]{0:T(1024)S(1)} %pad_clamp_fusion), kind=kCustom, calls=%fused_computation | custom fusion | bytes 14682112 | tf_op jit(solution)/shard_map/gather | solution.py:30
  519.0 8.9 %fusion = bf16[64,7168]{1,0:T(8,128)(2,1)S(1)} fusion(bf16[512,7168]{1,0:T(8,128)(2,1)} %gather_fusion, f32[64,8]{1,0:T(8,128)S(1)} %copy.47), kind=kLoop, calls=%fused_computation.2 | loop fusion | flops 10551296 | bytes 8259584 | tf_op jit(solution)/shard_map/reduce_sum | solution.py:32
  527.9 0.0 copy-start.1
  528.0 0.1 copy.55
  528.1 1.1 copy.48
  529.2 3.6 all-to-all-start.3
  532.7 0.0 reduce-scatter.4.cloned.1.call-done
  532.8 1.1 copy.53
  533.9 1.1 copy.49
  535.0 24.1 %all-to-all-done.3 = bf16[8,64,896]{2,1,0:T(8,128)(2,1)S(1)} async-done(((bf16[8,64,896]{2,1,0:T(8,128)(2,1)}), bf16[8,64,896]{2,1,0:T(8,128)(2,1)S(1)}, u32[]{:S(2)}, u32[]{:S(2)}) %all-to-all-start.3) | async-done | bytes 917536 | tf_op jit(solution)/shard_map/all_to_all | solution.py:16
  559.0 0.8 reduce_sum.48
  (14 shorter events, 0.1 us)
Async XLA Ops:
  7.2 3.2 copy-start
  276.2 7.4 %copy-start.2 = (bf16[32,20,7168]{2,0,1:T(8,128)(2,1)S(1)}, bf16[32,20,7168]{2,0,1:T(8,128)(2,1)}, u32[]{:S(2)}) copy-start(bf16[32,20,7168]{2,0,1:T(8,128)(2,1)} %reshape.134) | copy-start | bytes 27525124
  276.2 8.3 %copy-start.6 = (bf16[1,7168,256]{2,1,0:T(8,128)(2,1)S(1)}, bf16[1,7168,256]{2,1,0:T(8,128)(2,1)}, u32[]{:S(2)}) copy-start(bf16[1,7168,256]{2,1,0:T(8,128)(2,1)} %param.11) | copy-start | bytes 11010052
  284.5 2.5 copy-start.3
  305.9 8.2 %copy-start.4 = (bf16[1,1,64,7168]{3,2,1,0:T(8,128)(2,1)S(1)}, bf16[1,1,64,7168]{3,2,1,0:T(8,128)(2,1)}, u32[]{:S(2)}) copy-start(bf16[1,1,64,7168]{3,2,1,0:T(8,128)(2,1)} %param.13) | copy-start | bytes 2752516
  305.9 181.0 %all-to-all-start.2 = ((bf16[32,20,7168]{2,1,0:T(8,128)(2,1)}), bf16[32,20,7168]{2,1,0:T(8,128)(2,1)}, u32[]{:S(2)}, u32[]{:S(2)}) async-start(bf16[32,20,7168]{2,1,0:T(8,128)(2,1)} %copy.46), calls=%async_computation.2 | async-start | bytes 22020096 | tf_op jit(solution)/shard_map/all_to_all | solution.py:78
  314.1 218.6 %reduce-scatter.4.cloned.1.call-start = ((), (), s32[]{:S(2)}) async-start(), calls=%async_computation.5 | async-start | bytes 2064384
  314.2 3.1 copy-start.5
  527.9 31.9 %copy-start.1 = (bf16[64,7168]{1,0:T(8,128)(2,1)S(1)}, bf16[64,7168]{1,0:T(8,128)(2,1)}, u32[]{:S(2)}) copy-start(bf16[64,7168]{1,0:T(8,128)(2,1)} %param.7) | copy-start | bytes 2752516
  529.2 29.9 %all-to-all-start.3 = ((bf16[8,64,896]{2,1,0:T(8,128)(2,1)}), bf16[8,64,896]{2,1,0:T(8,128)(2,1)S(1)}, u32[]{:S(2)}, u32[]{:S(2)}) async-start(bf16[8,64,896]{2,1,0:T(8,128)(2,1)} %copy.48), calls=%async_computation.3 | async-start | bytes 1835008 | tf_op jit(solution)/shard_map/all_to_all | solution.py:16
Sparse Core Ops, SparseCore 0:
  317.5 33.5 reduce-scatter.3
